TPU v7x, 32 devices: a whole 2x2x4 slice. The times are simulated.
32 devices in a mesh: section: 4 (over z), tp: 4 (over y, core), dp: 2 (over x).
Axes of the slice: x: 2, y: 2, z: 4, core: 2. Of those that a mesh axis runs over, the one named last changes fastest.
Arguments:
- held: bfloat16 [4, 2, 128, 8192], P('section', 'dp', None, 'tp'), may hold values from -6 to 6
- incoming: bfloat16 [1, 2, 128, 8192], P(None, 'dp', None, 'tp'), may hold values from -6 to 6
- w_qkv: bfloat16 [4, 8192, 1536], P('section', None, 'tp'), may hold values from -0.0625 to 0.0625
- w_out: bfloat16 [4, 512, 8192], P('section', 'tp'), may hold values from -0.25 to 0.25
- norm_gain: bfloat16 [4, 8192], P('section'), may hold values from 0.099609375 to 1.8984375
Outputs:
- section_out: bfloat16 [2, 4, 2, 128, 8192], P(None, 'section', 'dp', None, 'tp')
- shadow_out: bfloat16 [2, 4, 2, 128, 8192], P(None, 'section', 'dp', None, 'tp')
All inputs are finite; a program needn't handle non-finite values.
Results may differ from a plain program's by a relative error of at most 0.014.
Values may be sent and summed in bfloat16 or wider, within the bound.
No kernel may reach another device: no remote copies, remote signals or barrier semaphores. Data moves between devices by JAX's collectives and lax.ppermute only.
A program may use at most 128 MiB of HBM per device.

v0:
```python
import jax
import jax.numpy as jnp
from jax import lax
from jax.sharding import PartitionSpec as P

HD = 128
TICKS = 2


EPS = 1e-05


def from_behind(x, axis, by):
    length = lax.axis_size(axis)
    return lax.ppermute(x, axis, [(i, (i + by) % length) for i in range(length)])


def shifted(block, axis, distance):
    devices = range(lax.axis_size(axis))
    route = [(i - distance, i) for i in devices if i - distance in devices]
    return lax.ppermute(block, axis, route)


def attend_layer(sharded, w_proj, w_out, gain_row):
    full = lax.all_gather(sharded, "tp", axis=2, tiled=True)
    batch, length, width = full.shape
    heads = w_proj.shape[1] // (3 * HD)
    values = full.astype(jnp.float32)
    scale = lax.rsqrt(jnp.mean(values * values, axis=-1, keepdims=True) + EPS)
    normed = (values * scale * gain_row.astype(jnp.float32)).astype(jnp.bfloat16)
    proj = jnp.dot(
        normed.reshape(batch * length, width), w_proj, preferred_element_type=jnp.float32
    )
    proj = proj.astype(jnp.bfloat16).reshape(batch, length, heads, 3, HD)
    query = proj[:, :, :, 0]
    key = proj[:, :, :, 1]
    value = proj[:, :, :, 2]
    scores = jnp.einsum("blhe,bmhe->bhlm", query, key, preferred_element_type=jnp.float32) * HD ** (
        -0.5
    )
    causal = jnp.arange(length)[:, None] >= jnp.arange(length)[None, :]
    scores = jnp.where(causal[None, None], scores, -1e30)
    weights = jax.nn.softmax(scores, axis=-1).astype(jnp.bfloat16)
    mixed = jnp.einsum("bhlm,bmhe->blhe", weights, value, preferred_element_type=jnp.float32)
    mixed = mixed.astype(jnp.bfloat16).reshape(batch * length, heads * HD)
    summed = jnp.dot(
        lax.all_gather(mixed, "tp", axis=1, tiled=True), w_out, preferred_element_type=jnp.float32
    )
    summed = summed.reshape(batch, length, w_out.shape[1])
    return (sharded.astype(jnp.float32) + summed).astype(jnp.bfloat16)


def local(held, incoming, w_qkv, w_out, norm_gain):
    position = lax.axis_index("section")
    own_proj = w_qkv[0]
    own_out = w_out[0]
    own_gain = norm_gain[0]
    own_out = lax.all_to_all(own_out, "tp", split_axis=1, concat_axis=0, tiled=True)
    current = held[0]
    next_proj, next_out, next_gain = from_behind((own_proj, own_out, own_gain), "section", -1)
    outputs = []
    shadows = []
    for tick in range(TICKS):
        result = attend_layer(current, own_proj, own_out, own_gain)
        outputs.append(result)
        shadows.append(attend_layer(result, next_proj, next_out, next_gain))
        if tick + 1 < TICKS:
            moved = shifted(result, "section", 1)
            current = jnp.where(position == 0, incoming[tick], moved)
    section_out = jnp.stack(outputs)[:, None]
    shadow_out = jnp.stack(shadows)[:, None]
    return (section_out, shadow_out)


def solution(mesh):
    placed = (
        P("section", "dp", None, "tp"),
        P(None, "dp", None, "tp"),
        P("section", None, "tp"),
        P("section", "tp", None),
        P("section", None),
    )
    return jax.shard_map(
        local,
        mesh=mesh,
        in_specs=placed,
        out_specs=(P(None, "section", "dp", None, "tp"), P(None, "section", "dp", None, "tp")),
        check_vma=False,
    )
```

profile of v0, /device:TPU:0, one launch (start us, length us, event | category | flops | bytes accessed | tf_op | source)
XLA Modules:
  0.0 311.9 jit_solution(6885120355747060948)
XLA Ops:
  7.9 4.1 %copy.31 = bf16[1,128,8192]{1,2,0:T(8,128)(2,1)} copy(bf16[1,128,8192]{2,1,0:T(8,128)(2,1)} %param.8) | data formatting | bytes 4194304 | tf_op args[3]
  12.0 4.3 %all-to-all-start = ((bf16[128,4,2048]{0,2,1:T(8,128)(2,1)}), bf16[128,4,2048]{0,2,1:T(8,128)(2,1)S(1)}, u32[]{:S(2)}, u32[]{:S(2)}) async-start(bf16[128,4,2048]{0,2,1:T(8,128)(2,1)} %bitcast.187), calls=%async_computation | async-start | bytes 4194304 | tf_op jit(solution)/shard_map/all_to_all | solution.py:58
  16.4 36.8 %all-to-all-done = bf16[128,4,2048]{0,2,1:T(8,128)(2,1)S(1)} async-done(((bf16[128,4,2048]{0,2,1:T(8,128)(2,1)}), bf16[128,4,2048]{0,2,1:T(8,128)(2,1)S(1)}, u32[]{:S(2)}, u32[]{:S(2)}) %all-to-all-start) | async-done | bytes 2097184 | tf_op jit(solution)/shard_map/all_to_all | solution.py:58
  54.5 2.9 copy.32
  57.4 2.1 fusion.6
  59.5 4.8 %fusion.43 = bf16[128,384]{1,0:T(8,128)(2,1)S(1)} fusion(bf16[1,1,128,8192]{3,2,1,0:T(8,128)(2,1)} %all-gather.15.cloned.1.call-done, f32[8192]{0:T(1024)S(1)} %convert_element_type.136, f32[128]{0:T(128)S(1)} %add_rsqrt_fusion.3, bf16[1,8192,384]{2,1,0:T(8,128)(2,1)} %param.7), kind=kOutput, calls=%fused_computation.47 | convolution fusion | flops 809549824 | bytes 8520192 | tf_op jit(solution)/shard_map/dot_general | solution.py:31
  64.9 5.4 %all-gather.1 = bf16[1,128,1,512]{1,3,2,0:T(8,128)(2,1)S(1)} all-gather(bf16[1,128,1,128]{1,3,2,0:T(8,128)(2,1)S(1)} %fusion.53), channel_id=3, replica_groups=mesh['section'=4,'tp'=4,'dp'=2] {'tp'}, dimensions={3}, use_global_device_ids=true | all-gather | bytes 163840 | tf_op jit(solution)/shard_map/all_gather | solution.py:47
  70.8 4.3 %collective-permute-start = (bf16[1,128,2048]{2,1,0:T(8,128)(2,1)S(1)}, bf16[1,128,2048]{2,1,0:T(8,128)(2,1)S(1)}, u32[]{:S(2)}, u32[]{:S(2)}) collective-permute-start(bf16[1,128,2048]{2,1,0:T(8,128)(2,1)S(1)} %bitcast.183), channel_id=1, source_target_pairs={{0,8},{8,16},{16,24},{1,9},{9,17},{17,25},{2,10},{10,18},{18,26},{... | collective-permute-start | bytes 1572872 | tf_op jit(solution)/shard_map/ppermute | solution.py:21
  75.1 11.6 %collective-permute-done = bf16[1,128,2048]{2,1,0:T(8,128)(2,1)S(1)} collective-permute-done((bf16[1,128,2048]{2,1,0:T(8,128)(2,1)S(1)}, bf16[1,128,2048]{2,1,0:T(8,128)(2,1)S(1)}, u32[]{:S(2)}, u32[]{:S(2)}) %collective-permute-start) | collective-permute-done | bytes 524320 | tf_op jit(solution)/shard_map/ppermute | solution.py:21
  88.7 4.6 %collective-permute-start.2 = (bf16[8192,384]{1,0:T(8,128)(2,1)}, bf16[8192,384]{1,0:T(8,128)(2,1)}, u32[]{:S(2)}, u32[]{:S(2)}) collective-permute-start(bf16[8192,384]{1,0:T(8,128)(2,1)} %bitcast.196), channel_id=1, source_target_pairs={{0,24},{8,0},{16,8},{24,16},{1,25},{9,1},{17,9},{25,17},{2,26},{10... | collective-permute-start | bytes 18874376 | tf_op jit(solution)/shard_map/ppermute | solution.py:15
  93.3 19.2 %all-gather.11.cloned.1.call-done = bf16[1,128,8192]{2,1,0:T(8,128)(2,1)} async-done(((bf16[1,128,2048]{2,1,0:T(8,128)(2,1)}), bf16[1,128,8192]{2,1,0:T(8,128)(2,1)}) %all-gather.11.cloned.1.call-update) | async-done | bytes 2097168 | tf_op jit(solution)/shard_map/all_gather | solution.py:25
  112.6 2.1 fusion
  114.7 4.8 %fusion.37 = bf16[128,384]{1,0:T(8,128)(2,1)S(1)} fusion(bf16[1,128,8192]{2,1,0:T(8,128)(2,1)} %all-gather.11.cloned.1.call-done, f32[128]{0:T(128)S(1)} %add_rsqrt_fusion.2, f32[8192]{0:T(1024)S(1)} %convert_element_type.136, bf16[1,8192,384]{2,1,0:T(8,128)(2,1)} %param.7), kind=kOutput, calls=%fused_computation.45 | convolution fusion | flops 809549824 | bytes 8520192 | tf_op jit(solution)/shard_map/dot_general | solution.py:31
  120.0 5.5 %all-gather.2 = bf16[1,128,1,512]{1,3,2,0:T(8,128)(2,1)S(1)} all-gather(bf16[1,128,1,128]{1,3,2,0:T(8,128)(2,1)S(1)} %fusion.54), channel_id=4, replica_groups=mesh['section'=4,'tp'=4,'dp'=2] {'tp'}, dimensions={3}, use_global_device_ids=true | all-gather | bytes 163840 | tf_op jit(solution)/shard_map/all_gather | solution.py:47
  126.7 3.4 %collective-permute-start.3 = (bf16[512,2048]{1,0:T(8,128)(2,1)S(1)}, bf16[512,2048]{1,0:T(8,128)(2,1)}, u32[]{:S(2)}, u32[]{:S(2)}) collective-permute-start(bf16[512,2048]{1,0:T(8,128)(2,1)S(1)} %bitcast.182), channel_id=1, source_target_pairs={{0,24},{8,0},{16,8},{24,16},{1,25},{9,1},{17,9},{25,17},{2,26},{10... | collective-permute-start | bytes 6291464 | tf_op jit(solution)/shard_map/ppermute | solution.py:15
  130.6 142.5 %collective-permute-done.1 = bf16[8192]{0:T(1024)(128)(2,1)S(1)} collective-permute-done((bf16[8192]{0:T(1024)(128)(2,1)S(1)}, bf16[8192]{0:T(1024)(128)(2,1)S(1)}, u32[]{:S(2)}, u32[]{:S(2)}) %collective-permute-start.1) | collective-permute-done | bytes 16416 | tf_op jit(solution)/shard_map/ppermute | solution.py:15
  273.2 2.1 fusion.9
  275.3 4.8 %fusion.46 = bf16[128,384]{1,0:T(8,128)(2,1)S(1)} fusion(bf16[8192,384]{1,0:T(8,128)(2,1)} %collective-permute-done.2, bf16[128,8192]{1,0:T(8,128)(2,1)} %all-gather.17.cloned.1.call-done, f32[8192]{0:T(1024)S(1)} %convert_element_type.156, f32[128]{0:T(128)S(1)} %add_rsqrt_fusion.1), kind=kOutput, calls=%fused_computation.48 | convolution fusion | flops 809549824 | bytes 8520192 | tf_op jit(solution)/shard_map/dot_general | solution.py:31
  280.6 5.6 %all-gather.4 = bf16[1,128,1,512]{1,3,2,0:T(8,128)(2,1)S(1)} all-gather(bf16[1,128,1,128]{1,3,2,0:T(8,128)(2,1)S(1)} %fusion.55), channel_id=6, replica_groups=mesh['section'=4,'tp'=4,'dp'=2] {'tp'}, dimensions={3}, use_global_device_ids=true | all-gather | bytes 163840 | tf_op jit(solution)/shard_map/all_gather | solution.py:47
  286.2 2.1 fusion.14
  289.4 2.1 fusion.3
  291.5 4.7 %fusion.40 = bf16[128,384]{1,0:T(8,128)(2,1)S(1)} fusion(bf16[8192,384]{1,0:T(8,128)(2,1)} %collective-permute-done.2, bf16[1,128,8192]{2,1,0:T(8,128)(2,1)} %all-gather.13.cloned.1.call-done, f32[128]{0:T(128)S(1)} %add_rsqrt_fusion, f32[8192]{0:T(1024)S(1)} %convert_element_type.156), kind=kOutput, calls=%fused_computation.46 | convolution fusion | flops 809549824 | bytes 8520192 | tf_op jit(solution)/shard_map/dot_general | solution.py:31
  296.8 5.4 %all-gather.5 = bf16[1,128,1,512]{1,3,2,0:T(8,128)(2,1)S(1)} all-gather(bf16[1,128,1,128]{1,3,2,0:T(8,128)(2,1)S(1)} %fusion.56), channel_id=7, replica_groups=mesh['section'=4,'tp'=4,'dp'=2] {'tp'}, dimensions={3}, use_global_device_ids=true | all-gather | bytes 163840 | tf_op jit(solution)/shard_map/all_gather | solution.py:47
  302.2 2.1 fusion.57
  (56 shorter events, 10.8 us)
Async XLA Ops:
  7.2 50.3 %all-gather.15.cloned.1.call-start = ((), (), s32[]{:S(2)}) async-start(), calls=%async_computation.3 | async-start | bytes 2621440 | tf_op jit(solution)/shard_map/all_gather | solution.py:25
  7.9 8.4 %copy-start.6 = (bf16[1,8192]{1,0:T(2,128)(2,1)S(1)}, bf16[1,8192]{1,0:T(2,128)(2,1)}, u32[]{:S(2)}) copy-start(bf16[1,8192]{1,0:T(2,128)(2,1)} %param.9) | copy-start | bytes 49156
  12.0 41.2 %all-to-all-start = ((bf16[128,4,2048]{0,2,1:T(8,128)(2,1)}), bf16[128,4,2048]{0,2,1:T(8,128)(2,1)S(1)}, u32[]{:S(2)}, u32[]{:S(2)}) async-start(bf16[128,4,2048]{0,2,1:T(8,128)(2,1)} %bitcast.187), calls=%async_computation | async-start | bytes 4194304 | tf_op jit(solution)/shard_map/all_to_all | solution.py:58
  16.3 96.3 %all-gather.11.cloned.1.call-start = ((), (), s32[]{:S(2)}) async-start(), calls=%async_computation.1 | async-start | bytes 2621440 | tf_op jit(solution)/shard_map/all_gather | solution.py:25
  53.2 1.3 copy-start.3
  59.5 10.8 %copy-start.5 = (bf16[1,1,128,2048]{3,2,1,0:T(8,128)(2,1)S(1)}, bf16[1,1,128,2048]{3,2,1,0:T(8,128)(2,1)}, u32[]{:S(2)}) copy-start(bf16[1,1,128,2048]{3,2,1,0:T(8,128)(2,1)} %param.5) | copy-start | bytes 1572868
  70.8 22.5 %copy-start = (bf16[128,2048]{1,0:T(8,128)(2,1)}, bf16[128,2048]{1,0:T(8,128)(2,1)S(1)}, u32[]{:S(2)}) copy-start(bf16[128,2048]{1,0:T(8,128)(2,1)S(1)} %fusion.12) | copy-start | bytes 1572868
  70.8 15.9 %collective-permute-start = (bf16[1,128,2048]{2,1,0:T(8,128)(2,1)S(1)}, bf16[1,128,2048]{2,1,0:T(8,128)(2,1)S(1)}, u32[]{:S(2)}, u32[]{:S(2)}) collective-permute-start(bf16[1,128,2048]{2,1,0:T(8,128)(2,1)S(1)} %bitcast.183), channel_id=1, source_target_pairs={{0,8},{8,16},{16,24},{1,9},{9,17},{17,25},{2,10},{10,18},{18,26},{... | collective-permute-start | bytes 1572872 | tf_op jit(solution)/shard_map/ppermute | solution.py:21
  88.6 184.5 %all-gather.17.cloned.1.call-start = ((), (), s32[]{:S(2)}) async-start(), calls=%async_computation.4 | async-start | bytes 2621440 | tf_op jit(solution)/shard_map/all_gather | solution.py:25
  88.7 186.6 %collective-permute-start.2 = (bf16[8192,384]{1,0:T(8,128)(2,1)}, bf16[8192,384]{1,0:T(8,128)(2,1)}, u32[]{:S(2)}, u32[]{:S(2)}) collective-permute-start(bf16[8192,384]{1,0:T(8,128)(2,1)} %bitcast.196), channel_id=1, source_target_pairs={{0,24},{8,0},{16,8},{24,16},{1,25},{9,1},{17,9},{25,17},{2,26},{10... | collective-permute-start | bytes 18874376 | tf_op jit(solution)/shard_map/ppermute | solution.py:15
  93.3 196.1 %all-gather.13.cloned.1.call-start = ((), (), s32[]{:S(2)}) async-start(), calls=%async_computation.2 | async-start | bytes 2621440 | tf_op jit(solution)/shard_map/all_gather | solution.py:25
  114.6 10.8 %copy-start.4 = (bf16[1,128,2048]{2,1,0:T(8,128)(2,1)S(1)}, bf16[1,128,2048]{2,1,0:T(8,128)(2,1)}, u32[]{:S(2)}) copy-start(bf16[1,128,2048]{2,1,0:T(8,128)(2,1)} %bitcast_select_fusion) | copy-start | bytes 1572868
  126.7 159.5 %collective-permute-start.3 = (bf16[512,2048]{1,0:T(8,128)(2,1)S(1)}, bf16[512,2048]{1,0:T(8,128)(2,1)}, u32[]{:S(2)}, u32[]{:S(2)}) collective-permute-start(bf16[512,2048]{1,0:T(8,128)(2,1)S(1)} %bitcast.182), channel_id=1, source_target_pairs={{0,24},{8,0},{16,8},{24,16},{1,25},{9,1},{17,9},{25,17},{2,26},{10... | collective-permute-start | bytes 6291464 | tf_op jit(solution)/shard_map/ppermute | solution.py:15
  130.1 143.0 %collective-permute-start.1 = (bf16[8192]{0:T(1024)(128)(2,1)S(1)}, bf16[8192]{0:T(1024)(128)(2,1)S(1)}, u32[]{:S(2)}, u32[]{:S(2)}) collective-permute-start(bf16[8192]{0:T(1024)(128)(2,1)S(1)} %reduce.20), channel_id=1, source_target_pairs={{0,24},{8,0},{16,8},{24,16},{1,25},{9,1},{17,9},{25,17},{2,26},{10... | collective-permute-start | bytes 49160 | tf_op jit(solution)/shard_map/ppermute | solution.py:15
  275.3 11.0 %copy-start.1 = (bf16[128,2048]{1,0:T(8,128)(2,1)S(1)}, bf16[128,2048]{1,0:T(8,128)(2,1)}, u32[]{:S(2)}) copy-start(bf16[128,2048]{1,0:T(8,128)(2,1)} %copy-done) | copy-start | bytes 1572868
  280.1 8.2 %copy-start.2 = (bf16[1,128,2048]{2,1,0:T(8,128)(2,1)S(1)}, bf16[1,128,2048]{2,1,0:T(8,128)(2,1)}, u32[]{:S(2)}) copy-start(bf16[1,128,2048]{2,1,0:T(8,128)(2,1)} %add_convert_fusion.1) | copy-start | bytes 1572868
Sparse Core Ops, SparseCore 0:
  9.5 36.6 all-gather.14
  88.8 23.7 all-gather.10
  114.7 22.5 all-gather.16
  139.3 22.5 all-gather.12
where the time goes:
time: 312 us
  waiting for transfers between devices  211 us (68%)
  matrix products  26.5 us (8%)
  blocking collectives  21.9 us (7%)
  starting transfers between devices  17.1 us (5%)
  between operations  13.9 us (4%)
  other arithmetic  12.6 us (4%)
  local copies, waits for them, and re-layouts  8.83 us (3%)
    ppermute x3, waiting for transfers between devices, from_behind(): lax.ppermute(x, axis, [(i, (i + by) % length) for i in range(length)])  143 us
    all_to_all x1, waiting for transfers between devices, local(): lax.all_to_all(own_out, 'tp', split_axis=1, concat_axis=0, tiled=True)  36.8 us
    all_gather x4, blocking collectives, attend_layer(): lax.all_gather(mixed, 'tp', axis=1, tiled=True)  21.9 us
    all_gather x4, waiting for transfers between devices, attend_layer(): full = lax.all_gather(sharded, 'tp', axis=2, tiled=True)  19.3 us
    dot_general x4, matrix products, attend_layer(): jnp.dot(normed.reshape(batch * length, width), w_proj, preferred_element_...  19.1 us
    ppermute x1, waiting for transfers between devices, shifted(): return lax.ppermute(block, axis, route)  11.6 us
    ppermute x3, starting transfers between devices, from_behind(): lax.ppermute(x, axis, [(i, (i + by) % length) for i in range(length)])  8.46 us
    reduce_sum x4, other arithmetic, attend_layer(): scale = lax.rsqrt(jnp.mean(values * values, axis=-1, keepdims=True) + EPS)  8.31 us
  transfers between devices with their start and end apart: 9, of which 4 were waited for; matrix products, arithmetic and copies ran while one was open for 8% of the time, Pallas kernels for 0%

commit v1 on v0

v1 whole, which is shorter than its diff:
```python
import functools

import jax
import jax.numpy as jnp
from jax import lax
from jax.experimental import pallas as pl
from jax.experimental.pallas import tpu as pltpu
from jax.sharding import PartitionSpec as P

HD = 128
TICKS = 2
EPS = 1e-05


def around(x, axis, by):
    length = lax.axis_size(axis)
    return lax.ppermute(x, axis, [(i, (i + by) % length) for i in range(length)])


def swapped(x, axis, bits):
    length = lax.axis_size(axis)
    return lax.ppermute(x, axis, [(i, i ^ bits) for i in range(length)])


def collected(block, axis):
    length = lax.axis_size(axis)
    pieces = {0: block}
    bit = length // 2
    while bit:
        pieces.update({k | bit: swapped(piece, axis, bit) for k, piece in list(pieces.items())})
        bit //= 2
    return [pieces[k] for k in range(length)]


def attend_body(place, *refs, count, sequences, width):
    pieces = refs[:count]
    w_ref, gain_ref, mixed_ref = refs[count : count + 3]
    x_buf, w_buf, x_sem, w_sem = refs[count + 3 :]
    mine = place[0]
    copies = []
    for k in range(count):
        rows = pl.ds((mine ^ k) * width, width)
        from_w = pltpu.make_async_copy(w_ref.at[rows], w_buf.at[k], w_sem.at[k])
        from_x = pltpu.make_async_copy(pieces[k], x_buf.at[k], x_sem.at[k])
        from_x.start()
        from_w.start()
        copies.append((from_x, from_w))
    total = None
    squares = None
    for k in range(count):
        copies[k][0].wait()
        values = x_buf[k].astype(jnp.float32)
        part = jnp.sum(values * values, axis=-1, keepdims=True)
        squares = part if squares is None else squares + part
        lifted = (values * gain_ref[mine ^ k].astype(jnp.float32)).astype(jnp.bfloat16)
        copies[k][1].wait()
        product = jnp.dot(lifted, w_buf[k], preferred_element_type=jnp.float32)
        total = product if total is None else total + product
    scale = lax.rsqrt(squares / (count * width) + EPS)
    proj = (total * scale).astype(jnp.bfloat16)
    heads = proj.shape[1] // (3 * HD)
    length = proj.shape[0] // sequences
    rows_at = lax.broadcasted_iota(jnp.int32, (length, length), 0)
    cols_at = lax.broadcasted_iota(jnp.int32, (length, length), 1)
    for b in range(sequences):
        for h in range(heads):
            part = proj[b * length : (b + 1) * length, h * 3 * HD : (h + 1) * 3 * HD]
            query, key, value = part[:, :HD], part[:, HD : 2 * HD], part[:, 2 * HD :]
            scores = lax.dot_general(
                query, key, (((1,), (1,)), ((), ())), preferred_element_type=jnp.float32
            ) * HD ** (-0.5)
            scores = jnp.where(rows_at >= cols_at, scores, -1e30)
            powers = jnp.exp(scores - jnp.max(scores, axis=-1, keepdims=True))
            weights = (powers / jnp.sum(powers, axis=-1, keepdims=True)).astype(jnp.bfloat16)
            mixed = jnp.dot(weights, value, preferred_element_type=jnp.float32)
            mixed_ref[b * length : (b + 1) * length, h * HD : (h + 1) * HD] = mixed.astype(
                jnp.bfloat16
            )


def attended(pieces, w_proj, gain_rows, place, sequences):
    count = len(pieces)
    rows, width = pieces[0].shape
    columns = w_proj.shape[1]
    anywhere = pl.BlockSpec(memory_space=pl.ANY)
    return pl.pallas_call(
        functools.partial(attend_body, count=count, sequences=sequences, width=width),
        out_shape=jax.ShapeDtypeStruct((rows, columns // 3), jnp.bfloat16),
        in_specs=[pl.BlockSpec(memory_space=pltpu.SMEM)]
        + [anywhere] * (count + 1)
        + [pl.BlockSpec(memory_space=pltpu.VMEM)],
        out_specs=pl.BlockSpec(memory_space=pltpu.VMEM),
        scratch_shapes=[
            pltpu.VMEM((count, rows, width), jnp.bfloat16),
            pltpu.VMEM((count, width, columns), jnp.bfloat16),
            pltpu.SemaphoreType.DMA((count,)),
            pltpu.SemaphoreType.DMA((count,)),
        ],
        name="attend",
    )(place, *pieces, w_proj, gain_rows)


def local(held, incoming, w_qkv, w_out, norm_gain):
    section = lax.axis_index("section")
    mine = lax.axis_index("tp")
    count = lax.axis_size("tp")
    _, sequences, length, width = held.shape
    rows = sequences * length
    w_proj = w_qkv[0]
    gain_rows = norm_gain.reshape(count, 1, width)
    place = mine.astype(jnp.int32).reshape(1)

    outs = []
    for k in range(count):
        wanted = lax.dynamic_slice_in_dim(w_out[0], (mine ^ k) * width, width, axis=1)
        outs.append(swapped(wanted, "tp", k) if k else wanted)
    out_columns = jnp.concatenate(outs, axis=0)

    def layer(block):
        mixed = attended(collected(block, "tp"), w_proj, gain_rows, place, sequences)
        mixed = jnp.concatenate(collected(mixed, "tp"), axis=1)
        added = jnp.dot(mixed, out_columns, preferred_element_type=jnp.float32)
        return (block.astype(jnp.float32) + added).astype(jnp.bfloat16)

    result = layer(held[0].reshape(rows, width))
    outputs = [result]
    shadows = []
    for tick in range(TICKS):
        layered = layer(around(result, "section", 1))
        shadows.append(around(layered, "section", -1))
        if tick + 1 < TICKS:
            fresh = layer(incoming[tick].reshape(rows, width))
            result = jnp.where(section == 0, fresh, layered)
            outputs.append(result)
    shape = (TICKS, 1, sequences, length, width)
    return (jnp.stack(outputs).reshape(shape), jnp.stack(shadows).reshape(shape))


def solution(mesh):
    placed = (
        P("section", "dp", None, "tp"),
        P(None, "dp", None, "tp"),
        P("section", None, "tp"),
        P("section", "tp", None),
        P("section", None),
    )
    out = P(None, "section", "dp", None, "tp")
    return jax.shard_map(
        local,
        mesh=mesh,
        in_specs=placed,
        out_specs=(out, out),
        check_vma=False,
    )
```

time: 312 us -> 183 us (0.59)
  waiting for transfers between devices: 211 us -> 125 us
  Pallas kernels: 0 us -> 24.4 us
  blocking collectives: 21.9 us -> 0 us
  matrix products: 26.5 us -> 7.7 us
  between operations: 13.9 us -> 0.99 us
  other arithmetic: 12.6 us -> 2.13 us
    all_to_all x1 -> x0, waiting for transfers between devices: 36.8 us -> none  [local(): lax.all_to_all(own_out, 'tp', split_axis=1, concat_axis=0, tiled=True)]
    ppermute x4 -> x31, waiting for transfers between devices: 154 us -> 125 us  [the longest x27 73.1 us: swapped(): return lax.ppermute(x, axis, [(i, i ^ bits) for i in range(length)])]
    pallas_call x0 -> x4, Pallas kernels: none -> 24.4 us  [attended(): pl.pallas_call(functools.partial(attend_body, count=count, sequences=sequ...]
    all_gather x4 -> x0, blocking collectives: 21.9 us -> none  [attend_layer(): lax.all_gather(mixed, 'tp', axis=1, tiled=True)]
    all_gather x4 -> x0, waiting for transfers between devices: 19.3 us -> none  [attend_layer(): full = lax.all_gather(sharded, 'tp', axis=2, tiled=True)]
    dot_general x16 -> x4, matrix products: 26.5 us -> 7.7 us  [layer(): added = jnp.dot(mixed, out_columns, preferred_element_type=jnp.float32)]
    reduce_sum x8 -> x0, other arithmetic: 8.48 us -> none  [the longest x4 8.31 us: attend_layer(): scale = lax.rsqrt(jnp.mean(values * values, axis=-1, keepdims=True) + EPS)]
    all_to_all x1 -> x0, starting transfers between devices: 4.26 us -> none  [local(): lax.all_to_all(own_out, 'tp', split_axis=1, concat_axis=0, tiled=True)]
  transfers between devices with their start and end apart: 9 -> 31, of which waited for: 4 -> 14; matrix products, arithmetic and copies ran while one was open for 8% -> 4% of each run, Pallas kernels for 0% -> 10%
where the time goes in v1:
time: 183 us; the launch traced here: 182 us
  waiting for transfers between devices  125 us (68%)
  Pallas kernels  24.4 us (13%)
  starting transfers between devices  16 us (9%)
  matrix products  7.7 us (4%)
  local copies, waits for them, and re-layouts  6.29 us (3%)
  other arithmetic  2.13 us (1%)
    ppermute x27, waiting for transfers between devices, swapped(): return lax.ppermute(x, axis, [(i, i ^ bits) for i in range(length)])  73.1 us
    ppermute x4, waiting for transfers between devices, around(): lax.ppermute(x, axis, [(i, (i + by) % length) for i in range(length)])  51.8 us
    pallas_call x4, Pallas kernels, attended(): pl.pallas_call(functools.partial(attend_body, count=count, sequences=sequ...  24.4 us
    ppermute x27, starting transfers between devices, swapped(): return lax.ppermute(x, axis, [(i, i ^ bits) for i in range(length)])  13.8 us
    dot_general x4, matrix products, layer(): added = jnp.dot(mixed, out_columns, preferred_element_type=jnp.float32)  7.7 us
  transfers between devices with their start and end apart: 31, of which 14 were waited for; matrix products, arithmetic and copies ran while one was open for 4% of the time, Pallas kernels for 10%

profile of v1, /device:TPU:0, one launch (start us, length us, event | category | flops | bytes accessed | tf_op | source)
XLA Modules:
  0.0 182.4 jit_solution(8154916668542367135)
XLA Ops:
  0.6 3.1 %collective-permute-start.1 = (bf16[128,2048]{1,0:T(8,128)(2,1)}, bf16[128,2048]{1,0:T(8,128)(2,1)S(1)}, u32[]{:S(2)}, u32[]{:S(2)}) collective-permute-start(bf16[128,2048]{1,0:T(8,128)(2,1)} %bitcast.35), channel_id=1, source_target_pairs={{0,4},{2,6},{4,0},{6,2},{1,5},{3,7},{5,1},{7,3},{8,12},{10,14},{12... | collective-permute-start | bytes 1572872 | tf_op jit(solution)/shard_map/ppermute | solution.py:22
  3.7 12.1 %collective-permute-done.1.refs_2_ = bf16[128,2048]{1,0:T(8,128)(2,1)S(1)} collective-permute-done((bf16[128,2048]{1,0:T(8,128)(2,1)}, bf16[128,2048]{1,0:T(8,128)(2,1)S(1)}, u32[]{:S(2)}, u32[]{:S(2)}) %collective-permute-start.1) | collective-permute-done | bytes 524320 | tf_op jit(solution)/shard_map/ppermute | solution.py:22
  15.8 2.9 %dynamic-slice_bitcast_fusion.3 = (bf16[128,2048]{1,0:T(8,128)(2,1)S(1)}, bf16[128,2048]{1,0:T(8,128)(2,1)}, bf16[128,2048]{1,0:T(8,128)(2,1)}, bf16[128,2048]{1,0:T(8,128)(2,1)S(1)}) fusion(bf16[1,128,8192]{2,1,0:T(8,128)(2,1)} %param.8, s32[]{:T(128)S(6)} %select_n.20, s32[]{:T(128)S(6)} %select_n.21, s32[]{:T(128)S(6)} %select_n.23, s32[]{:T(128)S(6)} %select_n.22), kind=kLoop, calls=%fused_computation.15 | loop fusion | bytes 4194320 | tf_op jit(solution)/shard_map/dynamic_slice | solution.py:115
  21.8 6.1 %attend.4 = bf16[128,128]{1,0:T(8,128)(2,1)} custom-call(s32[1]{0:T(128)} %bitcast.1.place, bf16[128,2048]{1,0:T(8,128)(2,1)} %bitcast.37, bf16[128,2048]{1,0:T(8,128)(2,1)} %copy-done.6, bf16[128,2048]{1,0:T(8,128)(2,1)} %copy-done.5, bf16[128,2048]{1,0:T(8,128)(2,1)} %copy-done.10, bf16[8192,384]{1,0:T(8,128)(2,1)} %bitcast.27, bf16[4,1,2048]{2,1,0:T(2,128)(2,1)} %bitcast.31), custom_call_target="tpu_custom_call" | custom-call | tf_op jit(solution)/shard_map/attend/pallas_call | solution.py:86
  28.0 1.8 collective-permute-start.4
  29.8 15.6 %collective-permute-done.4 = bf16[128,128]{1,0:T(8,128)(2,1)S(1)} collective-permute-done((bf16[128,128]{1,0:T(8,128)(2,1)}, bf16[128,128]{1,0:T(8,128)(2,1)S(1)}, u32[]{:S(2)}, u32[]{:S(2)}) %collective-permute-start.4) | collective-permute-done | bytes 32800 | tf_op jit(solution)/shard_map/ppermute | solution.py:22
  46.6 1.9 %fusion = bf16[128,2048]{1,0:T(8,128)(2,1)S(1)} fusion(bf16[128,128]{1,0:T(8,128)(2,1)S(1)} %collective-permute-done.5, bf16[128,128]{1,0:T(8,128)(2,1)S(1)} %collective-permute-done.4, bf16[128,128]{1,0:T(8,128)(2,1)S(1)} %collective-permute-done.3, bf16[128,128]{1,0:T(8,128)(2,1)} %attend.4, bf16[1,1,128,2048]{3,2,1,0:T(8,128)(2,1)S(1)} %copy-done, ...), kind=kOutput, calls=%fused_computation.4 | convolution fusion | flops 278134784 | bytes 3276800 | tf_op jit(solution)/shard_map/dot_general | solution.py:122
  48.5 1.8 %collective-permute-start.15 = (bf16[128,2048]{1,0:T(8,128)(2,1)S(1)}, bf16[128,2048]{1,0:T(8,128)(2,1)S(1)}, u32[]{:S(2)}, u32[]{:S(2)}) collective-permute-start(bf16[128,2048]{1,0:T(8,128)(2,1)S(1)} %fusion), channel_id=1, source_target_pairs={{0,8},{8,16},{16,24},{24,0},{1,9},{9,17},{17,25},{25,1},{2,10},{10... | collective-permute-start | bytes 1572872 | tf_op jit(solution)/shard_map/ppermute | solution.py:17
  50.4 14.3 %collective-permute-done.15.refs_0_ = bf16[128,2048]{1,0:T(8,128)(2,1)S(1)} collective-permute-done((bf16[128,2048]{1,0:T(8,128)(2,1)S(1)}, bf16[128,2048]{1,0:T(8,128)(2,1)S(1)}, u32[]{:S(2)}, u32[]{:S(2)}) %collective-permute-start.15) | collective-permute-done | bytes 524320 | tf_op jit(solution)/shard_map/ppermute | solution.py:17
  66.7 12.8 %collective-permute-done.17.refs_2_ = bf16[128,2048]{1,0:T(8,128)(2,1)S(1)} collective-permute-done((bf16[128,2048]{1,0:T(8,128)(2,1)S(1)}, bf16[128,2048]{1,0:T(8,128)(2,1)S(1)}, u32[]{:S(2)}, u32[]{:S(2)}) %collective-permute-start.17) | collective-permute-done | bytes 524320 | tf_op jit(solution)/shard_map/ppermute | solution.py:22
  79.9 9.3 %collective-permute-done.10.refs_2_ = bf16[128,2048]{1,0:T(8,128)(2,1)S(1)} collective-permute-done((bf16[128,2048]{1,0:T(8,128)(2,1)S(1)}, bf16[128,2048]{1,0:T(8,128)(2,1)S(1)}, u32[]{:S(2)}, u32[]{:S(2)}) %collective-permute-start.10) | collective-permute-done | bytes 524320 | tf_op jit(solution)/shard_map/ppermute | solution.py:22
  90.2 6.1 %attend.6 = bf16[128,128]{1,0:T(8,128)(2,1)} custom-call(s32[1]{0:T(128)} %bitcast.1.place, bf16[128,2048]{1,0:T(8,128)(2,1)} %copy-done.3, bf16[128,2048]{1,0:T(8,128)(2,1)} %copy-done.12, bf16[128,2048]{1,0:T(8,128)(2,1)} %copy-done.9, bf16[128,2048]{1,0:T(8,128)(2,1)} %collective-permute-done.18.refs_3_, bf16[8192,384]{1,0:T(8,128)(2,1)} %bitcast.28, ...), custom_call_target="tpu_custom_call" | custom-call | tf_op jit(solution)/shard_map/attend/pallas_call | solution.py:86
  98.5 6.1 %attend.5 = bf16[128,128]{1,0:T(8,128)(2,1)} custom-call(s32[1]{0:T(128)} %bitcast.1.place, bf16[128,2048]{1,0:T(8,128)(2,1)} %bitcast.38, bf16[128,2048]{1,0:T(8,128)(2,1)} %copy-done.11, bf16[128,2048]{1,0:T(8,128)(2,1)} %copy-done.8, bf16[128,2048]{1,0:T(8,128)(2,1)} %collective-permute-done.11.refs_3_, bf16[8192,384]{1,0:T(8,128)(2,1)} %bitcast.29, ...), custom_call_target="tpu_custom_call" | custom-call | tf_op jit(solution)/shard_map/attend/pallas_call | solution.py:86
  106.0 2.8 %collective-permute-done.13 = bf16[128,128]{1,0:T(8,128)(2,1)S(1)} collective-permute-done((bf16[128,128]{1,0:T(8,128)(2,1)}, bf16[128,128]{1,0:T(8,128)(2,1)S(1)}, u32[]{:S(2)}, u32[]{:S(2)}) %collective-permute-start.13) | collective-permute-done | bytes 32800 | tf_op jit(solution)/shard_map/ppermute | solution.py:22
  108.8 1.8 fusion.2
  110.7 2.0 %fusion.4 = bf16[128,2048]{1,0:T(8,128)(2,1)S(1)} fusion(bf16[128,2048]{1,0:T(8,128)(2,1)S(1)} %fusion.2, pred[]{:T(512)S(6)} %eq.3, bf16[128,128]{1,0:T(8,128)(2,1)S(1)} %collective-permute-done.14, bf16[128,128]{1,0:T(8,128)(2,1)S(1)} %collective-permute-done.13, bf16[128,128]{1,0:T(8,128)(2,1)S(1)} %collective-permute-done.12, ...), kind=kOutput, calls=%fused_computation.8 | convolution fusion | flops 278396928 | bytes 3801089 | tf_op jit(solution)/shard_map/dot_general | solution.py:122
  113.0 16.1 %collective-permute-done.23.refs_0_ = bf16[128,2048]{1,0:T(8,128)(2,1)S(1)} collective-permute-done((bf16[128,2048]{1,0:T(8,128)(2,1)S(1)}, bf16[128,2048]{1,0:T(8,128)(2,1)S(1)}, u32[]{:S(2)}, u32[]{:S(2)}) %collective-permute-start.23) | collective-permute-done | bytes 524320 | tf_op jit(solution)/shard_map/ppermute | solution.py:17
  129.8 12.8 %collective-permute-done.25.refs_2_ = bf16[128,2048]{1,0:T(8,128)(2,1)S(1)} collective-permute-done((bf16[128,2048]{1,0:T(8,128)(2,1)S(1)}, bf16[128,2048]{1,0:T(8,128)(2,1)S(1)}, u32[]{:S(2)}, u32[]{:S(2)}) %collective-permute-start.25) | collective-permute-done | bytes 524320 | tf_op jit(solution)/shard_map/ppermute | solution.py:22
  142.6 1.9 %collective-permute-done.26.refs_3_ = bf16[128,2048]{1,0:T(8,128)(2,1)S(1)} collective-permute-done((bf16[128,2048]{1,0:T(8,128)(2,1)S(1)}, bf16[128,2048]{1,0:T(8,128)(2,1)S(1)}, u32[]{:S(2)}, u32[]{:S(2)}) %collective-permute-start.26) | collective-permute-done | bytes 524320 | tf_op jit(solution)/shard_map/ppermute | solution.py:22
  145.3 6.1 %attend.7 = bf16[128,128]{1,0:T(8,128)(2,1)} custom-call(s32[1]{0:T(128)} %bitcast.1.place, bf16[128,2048]{1,0:T(8,128)(2,1)} %copy-done.7, bf16[128,2048]{1,0:T(8,128)(2,1)} %copy-done.14, bf16[128,2048]{1,0:T(8,128)(2,1)} %copy-done.13, bf16[128,2048]{1,0:T(8,128)(2,1)} %copy-done.15, bf16[8192,384]{1,0:T(8,128)(2,1)} %bitcast.30, bf16[4,1,2048]{2,1,0:T(2,128)(2,1)} %bitcast.34), custom_call_target="tpu_custom_call" | custom-call | tf_op jit(solution)/shard_map/attend/pallas_call | solution.py:86
  152.2 3.4 %collective-permute-done.28 = bf16[128,128]{1,0:T(8,128)(2,1)S(1)} collective-permute-done((bf16[128,128]{1,0:T(8,128)(2,1)}, bf16[128,128]{1,0:T(8,128)(2,1)S(1)}, u32[]{:S(2)}, u32[]{:S(2)}) %collective-permute-start.28) | collective-permute-done | bytes 32800 | tf_op jit(solution)/shard_map/ppermute | solution.py:22
  156.8 2.0 %fusion.3 = bf16[128,2048]{1,0:T(8,128)(2,1)S(1)} fusion(bf16[128,2048]{1,0:T(8,128)(2,1)} %copy-done.7, bf16[128,128]{1,0:T(8,128)(2,1)S(1)} %collective-permute-done.29, bf16[128,128]{1,0:T(8,128)(2,1)S(1)} %collective-permute-done.28, bf16[128,128]{1,0:T(8,128)(2,1)S(1)} %collective-permute-done.27, bf16[128,128]{1,0:T(8,128)(2,1)} %attend.7, ...), kind=kOutput, calls=%fused_computation.7 | convolution fusion | flops 278134784 | bytes 3276800 | tf_op jit(solution)/shard_map/dot_general | solution.py:122
  159.9 10.7 %collective-permute-done.22 = bf16[128,2048]{1,0:T(8,128)(2,1)S(1)} collective-permute-done((bf16[128,2048]{1,0:T(8,128)(2,1)}, bf16[128,2048]{1,0:T(8,128)(2,1)S(1)}, u32[]{:S(2)}, u32[]{:S(2)}) %collective-permute-start.22) | collective-permute-done | bytes 524320 | tf_op jit(solution)/shard_map/ppermute | solution.py:17
  170.6 10.8 %collective-permute-done.30 = bf16[128,2048]{1,0:T(8,128)(2,1)S(1)} collective-permute-done((bf16[128,2048]{1,0:T(8,128)(2,1)S(1)}, bf16[128,2048]{1,0:T(8,128)(2,1)S(1)}, u32[]{:S(2)}, u32[]{:S(2)}) %collective-permute-start.30) | collective-permute-done | bytes 524320 | tf_op jit(solution)/shard_map/ppermute | solution.py:17
  (95 shorter events, 17.2 us)
Async XLA Ops:
  0.6 15.2 %collective-permute-start.1 = (bf16[128,2048]{1,0:T(8,128)(2,1)}, bf16[128,2048]{1,0:T(8,128)(2,1)S(1)}, u32[]{:S(2)}, u32[]{:S(2)}) collective-permute-start(bf16[128,2048]{1,0:T(8,128)(2,1)} %bitcast.35), channel_id=1, source_target_pairs={{0,4},{2,6},{4,0},{6,2},{1,5},{3,7},{5,1},{7,3},{8,12},{10,14},{12... | collective-permute-start | bytes 1572872 | tf_op jit(solution)/shard_map/ppermute | solution.py:22
  3.7 17.2 %collective-permute-start = (bf16[128,2048]{1,0:T(8,128)(2,1)}, bf16[128,2048]{1,0:T(8,128)(2,1)S(1)}, u32[]{:S(2)}, u32[]{:S(2)}) collective-permute-start(bf16[128,2048]{1,0:T(8,128)(2,1)} %bitcast.36), channel_id=1, source_target_pairs={{0,2},{2,0},{4,6},{6,4},{1,3},{3,1},{5,7},{7,5},{8,10},{10,8},{12,... | collective-permute-start | bytes 1572872 | tf_op jit(solution)/shard_map/ppermute | solution.py:22
  15.8 5.0 %collective-permute-start.2 = (bf16[128,2048]{1,0:T(8,128)(2,1)S(1)}, bf16[128,2048]{1,0:T(8,128)(2,1)S(1)}, u32[]{:S(2)}, u32[]{:S(2)}) collective-permute-start(bf16[128,2048]{1,0:T(8,128)(2,1)S(1)} %collective-permute-done.1.refs_2_), channel_id=1, source_target_pairs={{0,2},{2,0},{4,6},{6,4},{1,3},{3,1},{5,7},{7,5},{8,10},{10,8},{12,... | collective-permute-start | bytes 1572872 | tf_op jit(solution)/shard_map/ppermute | solution.py:22
  18.7 26.7 %collective-permute-start.6 = (bf16[128,2048]{1,0:T(8,128)(2,1)}, bf16[128,2048]{1,0:T(8,128)(2,1)}, u32[]{:S(2)}, u32[]{:S(2)}) collective-permute-start(bf16[128,2048]{1,0:T(8,128)(2,1)} %get-tuple-element.5), channel_id=1, source_target_pairs={{0,2},{2,0},{4,6},{6,4},{1,3},{3,1},{5,7},{7,5},{8,10},{10,8},{12,... | collective-permute-start | bytes 1572872 | tf_op jit(solution)/shard_map/ppermute | solution.py:22
  19.0 26.4 %collective-permute-start.8 = (bf16[128,2048]{1,0:T(8,128)(2,1)}, bf16[128,2048]{1,0:T(8,128)(2,1)}, u32[]{:S(2)}, u32[]{:S(2)}) collective-permute-start(bf16[128,2048]{1,0:T(8,128)(2,1)} %get-tuple-element.6), channel_id=1, source_target_pairs={{0,6},{2,4},{4,2},{6,0},{1,7},{3,5},{5,3},{7,1},{8,14},{10,12},{12... | collective-permute-start | bytes 1572872 | tf_op jit(solution)/shard_map/ppermute | solution.py:22
  20.6 24.9 %collective-permute-start.7 = (bf16[128,2048]{1,0:T(8,128)(2,1)S(1)}, bf16[128,2048]{1,0:T(8,128)(2,1)}, u32[]{:S(2)}, u32[]{:S(2)}) collective-permute-start(bf16[128,2048]{1,0:T(8,128)(2,1)S(1)} %get-tuple-element.7), channel_id=1, source_target_pairs={{0,4},{2,6},{4,0},{6,2},{1,5},{3,7},{5,1},{7,3},{8,12},{10,14},{12... | collective-permute-start | bytes 1572872 | tf_op jit(solution)/shard_map/ppermute | solution.py:22
  28.0 17.4 %collective-permute-start.4 = (bf16[128,128]{1,0:T(8,128)(2,1)}, bf16[128,128]{1,0:T(8,128)(2,1)S(1)}, u32[]{:S(2)}, u32[]{:S(2)}) collective-permute-start(bf16[128,128]{1,0:T(8,128)(2,1)} %attend.4), channel_id=1, source_target_pairs={{0,4},{2,6},{4,0},{6,2},{1,5},{3,7},{5,1},{7,3},{8,12},{10,14},{12... | collective-permute-start | bytes 98312 | tf_op jit(solution)/shard_map/ppermute | solution.py:22
  29.8 15.6 %collective-permute-start.3 = (bf16[128,128]{1,0:T(8,128)(2,1)}, bf16[128,128]{1,0:T(8,128)(2,1)S(1)}, u32[]{:S(2)}, u32[]{:S(2)}) collective-permute-start(bf16[128,128]{1,0:T(8,128)(2,1)} %attend.4), channel_id=1, source_target_pairs={{0,2},{2,0},{4,6},{6,4},{1,3},{3,1},{5,7},{7,5},{8,10},{10,8},{12,... | collective-permute-start | bytes 98312 | tf_op jit(solution)/shard_map/ppermute | solution.py:22
  48.5 16.1 %collective-permute-start.15 = (bf16[128,2048]{1,0:T(8,128)(2,1)S(1)}, bf16[128,2048]{1,0:T(8,128)(2,1)S(1)}, u32[]{:S(2)}, u32[]{:S(2)}) collective-permute-start(bf16[128,2048]{1,0:T(8,128)(2,1)S(1)} %fusion), channel_id=1, source_target_pairs={{0,8},{8,16},{16,24},{24,0},{1,9},{9,17},{17,25},{25,1},{2,10},{10... | collective-permute-start | bytes 1572872 | tf_op jit(solution)/shard_map/ppermute | solution.py:17
  64.6 14.8 %collective-permute-start.17 = (bf16[128,2048]{1,0:T(8,128)(2,1)S(1)}, bf16[128,2048]{1,0:T(8,128)(2,1)S(1)}, u32[]{:S(2)}, u32[]{:S(2)}) collective-permute-start(bf16[128,2048]{1,0:T(8,128)(2,1)S(1)} %collective-permute-done.15.refs_0_), channel_id=1, source_target_pairs={{0,4},{2,6},{4,0},{6,2},{1,5},{3,7},{5,1},{7,3},{8,12},{10,14},{12... | collective-permute-start | bytes 1572872 | tf_op jit(solution)/shard_map/ppermute | solution.py:22
  66.2 23.1 %collective-permute-start.10 = (bf16[128,2048]{1,0:T(8,128)(2,1)S(1)}, bf16[128,2048]{1,0:T(8,128)(2,1)S(1)}, u32[]{:S(2)}, u32[]{:S(2)}) collective-permute-start(bf16[128,2048]{1,0:T(8,128)(2,1)S(1)} %bitcast.39), channel_id=1, source_target_pairs={{0,4},{2,6},{4,0},{6,2},{1,5},{3,7},{5,1},{7,3},{8,12},{10,14},{12... | collective-permute-start | bytes 1572872 | tf_op jit(solution)/shard_map/ppermute | solution.py:22
  66.7 22.6 %collective-permute-start.16 = (bf16[128,2048]{1,0:T(8,128)(2,1)S(1)}, bf16[128,2048]{1,0:T(8,128)(2,1)S(1)}, u32[]{:S(2)}, u32[]{:S(2)}) collective-permute-start(bf16[128,2048]{1,0:T(8,128)(2,1)S(1)} %collective-permute-done.15.refs_0_), channel_id=1, source_target_pairs={{0,2},{2,0},{4,6},{6,4},{1,3},{3,1},{5,7},{7,5},{8,10},{10,8},{12,... | collective-permute-start | bytes 1572872 | tf_op jit(solution)/shard_map/ppermute | solution.py:22
  79.4 9.9 %collective-permute-start.18 = (bf16[128,2048]{1,0:T(8,128)(2,1)S(1)}, bf16[128,2048]{1,0:T(8,128)(2,1)}, u32[]{:S(2)}, u32[]{:S(2)}) collective-permute-start(bf16[128,2048]{1,0:T(8,128)(2,1)S(1)} %collective-permute-done.17.refs_2_), channel_id=1, source_target_pairs={{0,2},{2,0},{4,6},{6,4},{1,3},{3,1},{5,7},{7,5},{8,10},{10,8},{12,... | collective-permute-start | bytes 1572872 | tf_op jit(solution)/shard_map/ppermute | solution.py:22
  79.4 18.3 %collective-permute-start.9 = (bf16[128,2048]{1,0:T(8,128)(2,1)S(1)}, bf16[128,2048]{1,0:T(8,128)(2,1)S(1)}, u32[]{:S(2)}, u32[]{:S(2)}) collective-permute-start(bf16[128,2048]{1,0:T(8,128)(2,1)S(1)} %bitcast.40), channel_id=1, source_target_pairs={{0,2},{2,0},{4,6},{6,4},{1,3},{3,1},{5,7},{7,5},{8,10},{10,8},{12,... | collective-permute-start | bytes 1572872 | tf_op jit(solution)/shard_map/ppermute | solution.py:22
  89.3 8.4 %collective-permute-start.11 = (bf16[128,2048]{1,0:T(8,128)(2,1)S(1)}, bf16[128,2048]{1,0:T(8,128)(2,1)}, u32[]{:S(2)}, u32[]{:S(2)}) collective-permute-start(bf16[128,2048]{1,0:T(8,128)(2,1)S(1)} %collective-permute-done.10.refs_2_), channel_id=1, source_target_pairs={{0,2},{2,0},{4,6},{6,4},{1,3},{3,1},{5,7},{7,5},{8,10},{10,8},{12,... | collective-permute-start | bytes 1572872 | tf_op jit(solution)/shard_map/ppermute | solution.py:22
  96.3 9.1 %collective-permute-start.20 = (bf16[128,128]{1,0:T(8,128)(2,1)}, bf16[128,128]{1,0:T(8,128)(2,1)S(1)}, u32[]{:S(2)}, u32[]{:S(2)}) collective-permute-start(bf16[128,128]{1,0:T(8,128)(2,1)} %attend.6), channel_id=1, source_target_pairs={{0,4},{2,6},{4,0},{6,2},{1,5},{3,7},{5,1},{7,3},{8,12},{10,14},{12... | collective-permute-start | bytes 98312 | tf_op jit(solution)/shard_map/ppermute | solution.py:22
  104.6 4.2 %collective-permute-start.13 = (bf16[128,128]{1,0:T(8,128)(2,1)}, bf16[128,128]{1,0:T(8,128)(2,1)S(1)}, u32[]{:S(2)}, u32[]{:S(2)}) collective-permute-start(bf16[128,128]{1,0:T(8,128)(2,1)} %attend.5), channel_id=1, source_target_pairs={{0,4},{2,6},{4,0},{6,2},{1,5},{3,7},{5,1},{7,3},{8,12},{10,14},{12... | collective-permute-start | bytes 98312 | tf_op jit(solution)/shard_map/ppermute | solution.py:22
  105.9 4.7 %collective-permute-start.12 = (bf16[128,128]{1,0:T(8,128)(2,1)}, bf16[128,128]{1,0:T(8,128)(2,1)S(1)}, u32[]{:S(2)}, u32[]{:S(2)}) collective-permute-start(bf16[128,128]{1,0:T(8,128)(2,1)} %attend.5), channel_id=1, source_target_pairs={{0,2},{2,0},{4,6},{6,4},{1,3},{3,1},{5,7},{7,5},{8,10},{10,8},{12,... | collective-permute-start | bytes 98312 | tf_op jit(solution)/shard_map/ppermute | solution.py:22
  112.7 16.4 %collective-permute-start.23 = (bf16[128,2048]{1,0:T(8,128)(2,1)S(1)}, bf16[128,2048]{1,0:T(8,128)(2,1)S(1)}, u32[]{:S(2)}, u32[]{:S(2)}) collective-permute-start(bf16[128,2048]{1,0:T(8,128)(2,1)S(1)} %fusion.4), channel_id=1, source_target_pairs={{0,8},{8,16},{16,24},{24,0},{1,9},{9,17},{17,25},{25,1},{2,10},{10... | collective-permute-start | bytes 1572872 | tf_op jit(solution)/shard_map/ppermute | solution.py:17
  129.1 13.5 %collective-permute-start.25 = (bf16[128,2048]{1,0:T(8,128)(2,1)S(1)}, bf16[128,2048]{1,0:T(8,128)(2,1)S(1)}, u32[]{:S(2)}, u32[]{:S(2)}) collective-permute-start(bf16[128,2048]{1,0:T(8,128)(2,1)S(1)} %collective-permute-done.23.refs_0_), channel_id=1, source_target_pairs={{0,4},{2,6},{4,0},{6,2},{1,5},{3,7},{5,1},{7,3},{8,12},{10,14},{12... | collective-permute-start | bytes 1572872 | tf_op jit(solution)/shard_map/ppermute | solution.py:22
  129.8 12.8 %collective-permute-start.24 = (bf16[128,2048]{1,0:T(8,128)(2,1)S(1)}, bf16[128,2048]{1,0:T(8,128)(2,1)S(1)}, u32[]{:S(2)}, u32[]{:S(2)}) collective-permute-start(bf16[128,2048]{1,0:T(8,128)(2,1)S(1)} %collective-permute-done.23.refs_0_), channel_id=1, source_target_pairs={{0,2},{2,0},{4,6},{6,4},{1,3},{3,1},{5,7},{7,5},{8,10},{10,8},{12,... | collective-permute-start | bytes 1572872 | tf_op jit(solution)/shard_map/ppermute | solution.py:22
  151.4 4.2 %collective-permute-start.28 = (bf16[128,128]{1,0:T(8,128)(2,1)}, bf16[128,128]{1,0:T(8,128)(2,1)S(1)}, u32[]{:S(2)}, u32[]{:S(2)}) collective-permute-start(bf16[128,128]{1,0:T(8,128)(2,1)} %attend.7), channel_id=1, source_target_pairs={{0,4},{2,6},{4,0},{6,2},{1,5},{3,7},{5,1},{7,3},{8,12},{10,14},{12... | collective-permute-start | bytes 98312 | tf_op jit(solution)/shard_map/ppermute | solution.py:22
  155.6 15.0 %collective-permute-start.22 = (bf16[128,2048]{1,0:T(8,128)(2,1)}, bf16[128,2048]{1,0:T(8,128)(2,1)S(1)}, u32[]{:S(2)}, u32[]{:S(2)}) collective-permute-start(bf16[128,2048]{1,0:T(8,128)(2,1)} %copy-done.22), channel_id=1, source_target_pairs={{0,24},{8,0},{16,8},{24,16},{1,25},{9,1},{17,9},{25,17},{2,26},{10... | collective-permute-start | bytes 1572872 | tf_op jit(solution)/shard_map/ppermute | solution.py:17
  158.8 22.6 %collective-permute-start.30 = (bf16[128,2048]{1,0:T(8,128)(2,1)S(1)}, bf16[128,2048]{1,0:T(8,128)(2,1)S(1)}, u32[]{:S(2)}, u32[]{:S(2)}) collective-permute-start(bf16[128,2048]{1,0:T(8,128)(2,1)S(1)} %fusion.3), channel_id=1, source_target_pairs={{0,24},{8,0},{16,8},{24,16},{1,25},{9,1},{17,9},{25,17},{2,26},{10... | collective-permute-start | bytes 1572872 | tf_op jit(solution)/shard_map/ppermute | solution.py:17
  (30 other events, 285.6 us)
